TPU v7x, 256 devices: a whole 4x4x8 slice. The times are simulated.
256 devices in a mesh: expert: 4 (over y), shard: 64 (over z, x, core).
Axes of the slice: x: 4, y: 4, z: 8, core: 2. Of those that a mesh axis runs over, the one named last changes fastest.
Arguments:
- gradient: bfloat16 [4, 2048, 28672], P('expert', 'shard'), may hold values from -16 to 16
- factor: float32 [4, 2048, 512], P('expert', 'shard'), may hold values from -2 to 2, as said below
- right_diag: float32 [4, 28672], P('expert', 'shard'), may hold values from 0.5 to 2
- counts: int32 [4], P('expert'), may hold values from 256 to 1023
Outputs:
- new_factor: float32 [4, 2048, 512], P('expert', 'shard')
- new_right: float32 [4, 28672], P('expert', 'shard')
Inputs may be any that keep to these rules, and one draw needn't show every extreme that they name: Every diagonal block of factor is upper triangular with a positive diagonal: in row r, entry j is zero for j < r % 512.
All inputs are finite; a program needn't handle non-finite values. Where the computation divides by a largest or mean magnitude, that divisor is 1e-20 or more.
Results may differ from a plain program's by a relative error of at most 0.002.
Values may be sent and summed in bfloat16 or wider, within the bound.
No kernel may reach another device: no remote copies, remote signals or barrier semaphores. Data moves between devices by JAX's collectives and lax.ppermute only.
A program may use at most 128 MiB of HBM per device.

v0:
```python
import jax
import jax.numpy as jnp
from jax import lax
from jax.sharding import Mesh
from jax.sharding import PartitionSpec as P

FF = 14336
SHARD = ("shard_0", "shard_1", "shard_2")
step_rate = 0.5
epsilon = 1e-06


def from_everyone(shard, axis):
    size = lax.axis_size(axis)
    return lax.all_to_all(
        jnp.broadcast_to(shard[None], (size, *shard.shape)), axis, 0, 0, tiled=True
    )


def of_everyone(shard, axis):
    everything = from_everyone(shard, axis)
    return jnp.sum(everything, axis=0)


def cut_along(shard, dim, size):
    before, after = (shard.shape[:dim], shard.shape[dim + 1 :])
    return jnp.moveaxis(shard.reshape(*before, size, -1, *after), dim, 0)


def laid_out(parts, dim):
    shape = list(parts.shape[1:])
    shape[dim] *= parts.shape[0]
    return jnp.moveaxis(parts, 0, dim).reshape(shape)


def moved_by_axis(parts, axes, sequence):
    inside = parts.shape[1:]
    out = parts.reshape(*(lax.axis_size(a) for a in axes), *inside)
    for k in sequence:
        out = lax.all_to_all(out, axes[k], k, k, tiled=True)
    return out.reshape(-1, *inside)


def two_step_exchange(shard, groups, sequence, split_dim, concat_dim):
    size = lax.axis_size(groups[0]) * lax.axis_size(groups[1])
    parts = cut_along(shard, split_dim, size)
    return laid_out(moved_by_axis(parts, groups, sequence), concat_dim)


def all_blocks(shard, axes, sequence):
    parts = shard[None]
    for k in sequence:
        parts = lax.all_gather(parts, axes[k], axis=0, tiled=True)
    held = [lax.axis_size(axes[k]) for k in reversed(sequence)]
    parts = parts.reshape(*held, *shard.shape)
    turned = sorted(range(len(sequence)), key=lambda place: sequence[len(sequence) - 1 - place])
    return parts.transpose(*turned, *range(len(sequence), parts.ndim)).reshape(-1, *shard.shape)


def gather_axes(shard, axes, sequence, dim):
    return laid_out(all_blocks(shard, axes, sequence), dim)


def sum_by_axis(so_far, axes):
    for axis in axes:
        so_far = lax.psum_scatter(so_far, axis, scatter_dimension=0, tiled=True)
    return so_far


def of_everyone_2(shard, axis):
    return from_everyone(shard, axis).max(axis=0)


def in_one(arrays, axis):
    ends = [0]
    for a in arrays:
        ends.append(ends[-1] + a.size)
    so_far = of_everyone_2(jnp.concatenate([a.ravel() for a in arrays]), axis)
    return tuple((so_far[b:e].reshape(a.shape) for a, b, e in zip(arrays, ends, ends[1:])))


def body(gradient, factor, right_diag, counts):
    local_experts = counts.shape[0]
    experts_all = local_experts * lax.axis_size("expert")
    token_sum = of_everyone(jnp.sum(counts), "expert")
    weight = experts_all * counts.astype(jnp.float32) / jnp.asarray(token_sum).astype(jnp.float32)
    squared = weight * weight
    columns = two_step_exchange(gradient, (("shard_0", "shard_1"), "shard_2"), (1, 0), 2, 1)
    own_rows = factor.shape[1]
    block = factor.shape[2]
    width = columns.shape[1]
    col_count = columns.shape[2]
    narrow = factor.astype(jnp.bfloat16)
    whole = gather_axes(narrow, SHARD, (1, 0, 2), 1)
    blocks = width // block
    left = whole.reshape((local_experts, blocks, block, block))
    right = columns.reshape((local_experts, blocks, block, col_count))
    raw = jnp.einsum("ebik,ebkc->ebic", left, right, preferred_element_type=jnp.float32)
    raw = raw.reshape((local_experts, width, col_count))
    image = (raw * right_diag[:, None, :]).astype(jnp.bfloat16)
    column_term = (
        squared[:, None] * jnp.sum(jnp.square(image.astype(jnp.float32)), axis=1) / width - 1.0
    )
    column_level = jnp.max(jnp.abs(column_term), axis=1)
    groups = own_rows * lax.axis_size(SHARD) // own_rows

    def one_group(group):
        begin = group * own_rows
        picked = lax.dynamic_slice_in_dim(image, begin, own_rows, 1)
        window = lax.dynamic_slice_in_dim(image, begin // block * block, block, 1)
        return jnp.einsum("eic,ejc->iej", picked, window, preferred_element_type=jnp.float32)

    parts = lax.map(one_group, jnp.arange(groups, dtype=jnp.int32))
    gram = sum_by_axis(
        parts.reshape((own_rows * lax.axis_size(SHARD), local_experts, block)), SHARD
    )
    gram = jnp.transpose(gram, (1, 0, 2)) * (squared / (2 * FF))[:, None, None]
    my_index = lax.axis_index(SHARD)
    first_row = my_index * own_rows
    row_place = (first_row + lax.broadcasted_iota(jnp.int32, (own_rows, block), 0)) % block
    col_place = lax.broadcasted_iota(jnp.int32, (own_rows, block), 1)
    identity = jnp.where(col_place == row_place, 1.0, 0.0).astype(jnp.float32)
    upper_part = jnp.where((col_place >= row_place)[None, :, :], gram - identity[None, :, :], 0.0)
    row_level = jnp.max(jnp.abs(upper_part), axis=(1, 2))
    row_peak, column_peak = in_one((row_level, column_level), SHARD)
    steps = (upper_part / (row_peak + epsilon)[:, None, None]).astype(jnp.bfloat16)
    diag_block = lax.dynamic_slice_in_dim(whole, first_row // block * block, block, 1)
    moved = jnp.einsum("eik,ekj->eij", steps, diag_block, preferred_element_type=jnp.float32)
    new_factor = factor - step_rate * moved
    new_right = right_diag - step_rate * column_term / (column_peak + epsilon)[:, None] * right_diag
    return (new_factor, new_right)


def solution(mesh):
    torus = Mesh(
        mesh.devices.reshape(mesh.shape["expert"], 8, 4, 2),
        ("expert", "shard_0", "shard_1", "shard_2"),
    )
    return jax.shard_map(
        body,
        mesh=torus,
        in_specs=(
            P("expert", SHARD, None),
            P("expert", SHARD, None),
            P("expert", SHARD),
            P("expert"),
        ),
        out_specs=(P("expert", SHARD, None), P("expert", SHARD)),
        check_vma=False,
    )
```

profile of v0, /device:TPU:1, one launch (start us, length us, event | category | flops | bytes accessed | tf_op | source)
XLA Modules:
  0.0 385.5 jit_solution(12259285968247481593)
XLA Ops:
  8.1 11.3 %all-gather = bf16[4,32,512]{2,1,0:T(8,128)(2,1)} all-gather(bf16[1,32,512]{2,1,0:T(8,128)(2,1)S(1)} %convert_element_type.51), channel_id=2, replica_groups=mesh['expert'=4,'shard_0'=8,'shard_1'=4,'shard_2'=2] {'shard_1'}, dimensions={0}, use_global_device_ids=true | all-gather | bytes 163840 | tf_op jit(solution)/shard_map/all_gather | solution.py:53
  19.4 3.6 reshape.312
  23.0 1.2 copy.38
  24.4 9.7 %all_to_all.22 = bf16[32,2,1,32,448]{4,3,0,2,1:T(8,128)(2,1)S(1)} all-to-all(bf16[32,2,1,32,448]{4,3,0,2,1:T(8,128)(2,1)S(1)} %copy.39), channel_id=1, replica_groups=mesh['expert'=4,'shard_0'=8,'shard_1'=4,'shard_2'=2] {'shard_2'}, dimensions={1} | all-to-all | bytes 3670016 | tf_op jit(solution)/shard_map/all_to_all | solution.py:40
  34.2 1.6 copy.40
  35.8 9.1 %all-to-all-start.1 = ((bf16[32,2,1,32,448]{4,3,1,2,0:T(8,128)(2,1)}), bf16[32,2,1,32,448]{4,3,1,2,0:T(8,128)(2,1)}, u32[]{:S(2)}, u32[]{:S(2)}) async-start(bf16[32,2,1,32,448]{4,3,1,2,0:T(8,128)(2,1)} %copy.40), calls=%async_computation.1 | async-start | bytes 4194304 | tf_op jit(solution)/shard_map/all_to_all | solution.py:40
  44.9 21.0 %all-gather.6.cloned.1.call-done = bf16[32,32,512]{2,1,0:T(8,128)(2,1)} async-done(((bf16[4,32,512]{2,1,0:T(8,128)(2,1)}), bf16[32,32,512]{2,1,0:T(8,128)(2,1)}) %all-gather.6.cloned.1.call-update) | async-done | bytes 1048592 | tf_op jit(solution)/shard_map/all_gather | solution.py:53
  66.1 22.5 %all-gather.8.cloned.1.call-done = bf16[64,32,512]{2,1,0:T(8,128)(2,1)} async-done(((bf16[32,32,512]{2,1,0:T(8,128)(2,1)}), bf16[64,32,512]{2,1,0:T(8,128)(2,1)}) %all-gather.8.cloned.1.call-update) | async-done | bytes 2097168 | tf_op jit(solution)/shard_map/all_gather | solution.py:53
  88.5 1.7 copy.37
  90.3 8.6 %all-to-all-done.1 = bf16[32,2,1,32,448]{4,3,1,2,0:T(8,128)(2,1)} async-done(((bf16[32,2,1,32,448]{4,3,1,2,0:T(8,128)(2,1)}), bf16[32,2,1,32,448]{4,3,1,2,0:T(8,128)(2,1)}, u32[]{:S(2)}, u32[]{:S(2)}) %all-to-all-start.1) | async-done | bytes 1835040 | tf_op jit(solution)/shard_map/all_to_all | solution.py:40
  98.9 2.9 multiply_reduce_fusion
  101.8 4.3 %copy.42 = f32[4,512,448]{1,0,2:T(4,128)} copy(f32[4,512,448]{1,2,0:T(8,128)S(1)} %get-tuple-element.92) | data formatting | bytes 7340032 | tf_op jit(solution)/shard_map/ebik,ebkc->ebic/dot_general | solution.py:98
  106.1 5.5 %reshape.315 = f32[1,2048,448]{1,2,0:T(8,128)} reshape(f32[4,512,448]{1,0,2:T(4,128)} %copy.42) | data formatting | bytes 7340032 | tf_op jit(solution)/shard_map/reshape | solution.py:99
  111.6 3.6 multiply_convert_fusion.1
  115.2 2.8 copy.43
  118.0 138.5 %while.12 = (s32[]{:T(128)}, f32[64,32,1,512]{3,1,2,0:T(8,128)}, s32[64]{0:T(128)S(1)}, bf16[1,2048,448]{2,1,0:T(8,128)(2,1)S(1)}, s32[]{:T(128)}, /*index=5*/s3...) while((s32[]{:T(128)}, f32[64,32,1,512]{3,1,2,0:T(8,128)}, ...), condition=%wide.region_1.0_spmd, body=%wide.region_0.0_spmd.sunk | while | flops 14680088 | bytes 623474 | solution.py:113
  121.4 0.9 fusion.36
  123.6 0.9 fusion.36
  134.4 0.9 fusion.36
  136.6 0.9 fusion.36
  143.1 0.9 fusion.36
  147.4 0.9 fusion.36
  149.6 0.9 fusion.36
  151.7 0.9 fusion.36
  179.8 0.9 fusion.36
  186.3 0.9 fusion.36
  188.5 0.9 fusion.36
  197.1 0.9 fusion.36
  201.5 0.9 fusion.36
  203.6 0.9 fusion.36
  208.0 0.9 fusion.36
  216.6 0.9 fusion.36
  218.8 0.9 fusion.36
  223.1 0.9 fusion.36
  231.8 0.9 fusion.36
  233.9 0.9 fusion.36
  238.3 0.9 fusion.36
  251.2 0.9 fusion.36
  255.6 0.9 fusion.36
  256.5 54.2 %reduce-scatter.4.cloned.1.call-done = f32[256,1,512]{2,0,1:T(8,128)} async-done(((f32[2048,1,512]{2,0,1:T(8,128)}), f32[256,1,512]{2,0,1:T(8,128)}) %reduce-scatter.4.cloned.1.call-update) | async-done | bytes 524304 | tf_op jit(solution)/shard_map/reduce_scatter | solution.py:66
  312.0 4.0 %all-to-all-start.2 = ((s32[4,1,1]{2,1,0:T(1,128)}), s32[4,1,1]{2,1,0:T(1,128)S(1)}, u32[]{:S(2)}, u32[]{:S(2)}) async-start(s32[4,1,1]{2,1,0:T(1,128)} %broadcast_in_dim.51), calls=%async_computation.5 | async-start | bytes 4096 | tf_op jit(solution)/shard_map/all_to_all | solution.py:15
  316.0 17.7 %reduce-scatter.6.cloned.1.call-done = f32[64,1,512]{2,0,1:T(8,128)} async-done(((f32[256,1,512]{2,0,1:T(8,128)}), f32[64,1,512]{2,0,1:T(8,128)}) %reduce-scatter.6.cloned.1.call-update) | async-done | bytes 131088 | tf_op jit(solution)/shard_map/reduce_scatter | solution.py:66
  335.7 16.1 %reduce-scatter.8.cloned.1.call-done = f32[32,1,512]{2,0,1:T(8,128)} async-done(((f32[64,1,512]{2,0,1:T(8,128)}), f32[32,1,512]{2,0,1:T(8,128)}) %reduce-scatter.8.cloned.1.call-update) | async-done | bytes 65552 | tf_op jit(solution)/shard_map/reduce_scatter | solution.py:66
  351.8 1.5 fusion.12
  353.4 1.3 pad_maximum_fusion
  355.3 9.9 %all-to-all-start.3 = ((f32[64,1,2]{2,1,0:T(1,128)}), f32[64,1,2]{2,1,0:T(1,128)S(1)}, u32[]{:S(2)}, u32[]{:S(2)}) async-start(f32[64,1,2]{2,1,0:T(1,128)} %broadcast_in_dim.56), calls=%async_computation.6 | async-start | bytes 65536 | tf_op jit(solution)/shard_map/all_to_all | solution.py:15
  365.2 9.3 %all-to-all-done.3 = f32[64,1,2]{2,1,0:T(1,128)S(1)} async-done(((f32[64,1,2]{2,1,0:T(1,128)}), f32[64,1,2]{2,1,0:T(1,128)S(1)}, u32[]{:S(2)}, u32[]{:S(2)}) %all-to-all-start.3) | async-done | bytes 544 | tf_op jit(solution)/shard_map/all_to_all | solution.py:15
  377.0 2.0 fusion.7
  (136 shorter events, 79.1 us)
Async XLA Ops:
  7.2 58.8 %all-gather.6.cloned.1.call-start = ((), (), s32[]{:S(2)}) async-start(), calls=%async_computation.10 | async-start | bytes 1179648 | tf_op jit(solution)/shard_map/all_gather | solution.py:53
  35.8 63.1 %all-to-all-start.1 = ((bf16[32,2,1,32,448]{4,3,1,2,0:T(8,128)(2,1)}), bf16[32,2,1,32,448]{4,3,1,2,0:T(8,128)(2,1)}, u32[]{:S(2)}, u32[]{:S(2)}) async-start(bf16[32,2,1,32,448]{4,3,1,2,0:T(8,128)(2,1)} %copy.40), calls=%async_computation.1 | async-start | bytes 4194304 | tf_op jit(solution)/shard_map/all_to_all | solution.py:40
  44.9 43.7 %all-gather.8.cloned.1.call-start = ((), (), s32[]{:S(2)}) async-start(), calls=%async_computation.11 | async-start | bytes 3145728 | tf_op jit(solution)/shard_map/all_gather | solution.py:53
  66.0 244.8 %reduce-scatter.4.cloned.1.call-start = ((), (), s32[]{:S(2)}) async-start(), calls=%async_computation.7 | async-start | bytes 4718592 | tf_op jit(solution)/shard_map/reduce_scatter | solution.py:66
  88.5 10.3 %copy-start.2 = (f32[1,448]{1,0:T(1,128)S(1)}, f32[1,448]{1,0:T(1,128)}, u32[]{:S(2)}) copy-start(f32[1,448]{1,0:T(1,128)} %param.8) | copy-start | bytes 5380
  90.3 11.5 %copy-start = (bf16[2,8,4,1,32,512]{5,4,0,2,1,3:T(8,128)(2,1)}, bf16[2,8,4,1,32,512]{5,4,0,2,1,3:T(8,128)(2,1)S(1)}, u32[]{:S(2)}) copy-start(bf16[2,8,4,1,32,512]{5,4,0,2,1,3:T(8,128)(2,1)S(1)} %copy.37) | copy-start | bytes 6291460
  256.5 120.6 %copy-start.1 = (f32[1,32,512]{2,1,0:T(8,128)S(1)}, f32[1,32,512]{2,1,0:T(8,128)}, u32[]{:S(2)}) copy-start(f32[1,32,512]{2,1,0:T(8,128)} %param.7) | copy-start | bytes 196612
  256.5 77.2 %reduce-scatter.6.cloned.1.call-start = ((), (), s32[]{:S(2)}) async-start(), calls=%async_computation.8 | async-start | bytes 655360 | tf_op jit(solution)/shard_map/reduce_scatter | solution.py:66
  312.0 21.7 %all-to-all-start.2 = ((s32[4,1,1]{2,1,0:T(1,128)}), s32[4,1,1]{2,1,0:T(1,128)S(1)}, u32[]{:S(2)}, u32[]{:S(2)}) async-start(s32[4,1,1]{2,1,0:T(1,128)} %broadcast_in_dim.51), calls=%async_computation.5 | async-start | bytes 4096 | tf_op jit(solution)/shard_map/all_to_all | solution.py:15
  316.0 35.8 %reduce-scatter.8.cloned.1.call-start = ((), (), s32[]{:S(2)}) async-start(), calls=%async_computation.9 | async-start | bytes 196608 | tf_op jit(solution)/shard_map/reduce_scatter | solution.py:66
  355.3 19.2 %all-to-all-start.3 = ((f32[64,1,2]{2,1,0:T(1,128)}), f32[64,1,2]{2,1,0:T(1,128)S(1)}, u32[]{:S(2)}, u32[]{:S(2)}) async-start(f32[64,1,2]{2,1,0:T(1,128)} %broadcast_in_dim.56), calls=%async_computation.6 | async-start | bytes 65536 | tf_op jit(solution)/shard_map/all_to_all | solution.py:15
Sparse Core Ops, SparseCore 0:
  19.5 46.4 all-gather.5
  67.8 20.7 all-gather.7
  256.6 54.1 reduce-scatter.3
  313.2 20.4 reduce-scatter.5
  336.0 15.7 reduce-scatter.7
where the time goes:
time: 387 us; the launch traced here: 386 us
  waiting for transfers between devices  149 us (39%)
  matrix products  62.5 us (16%)
  local copies, waits for them, and re-layouts  60 us (16%)
  loops' own time  43.6 us (11%)
  starting transfers between devices  23.2 us (6%)
  blocking collectives  21.1 us (5%)
  between operations  16.5 us (4%)
  other arithmetic  9.29 us (2%)
    reduce_scatter x3, waiting for transfers between devices, sum_by_axis(): so_far = lax.psum_scatter(so_far, axis, scatter_dimension=0, tiled=True)  88 us
    dot_general x64, matrix products, one_group(): jnp.einsum('eic,ejc->iej', picked, window, preferred_element_type=jnp.flo...  57.6 us
    another operation x1, loops' own time, body(): parts = lax.map(one_group, jnp.arange(groups, dtype=jnp.int32))  43.6 us
    all_gather x2, waiting for transfers between devices, all_blocks(): parts = lax.all_gather(parts, axes[k], axis=0, tiled=True)  43.5 us
    dynamic_slice x64, local copies, waits for them, and re-layouts, body(): parts = lax.map(one_group, jnp.arange(groups, dtype=jnp.int32))  37.3 us
    all_to_all x2, starting transfers between devices, from_everyone(): lax.all_to_all(jnp.broadcast_to(shard[None], (size, *shard.shape)), axis,...  13.9 us
    all_gather x1, blocking collectives, all_blocks(): parts = lax.all_gather(parts, axes[k], axis=0, tiled=True)  11.3 us
    all_to_all x1, blocking collectives, moved_by_axis(): out = lax.all_to_all(out, axes[k], k, k, tiled=True)  9.74 us
  transfers between devices with their start and end apart: 8, of which 7 were waited for; matrix products, arithmetic and copies ran while one was open for 3% of the time, Pallas kernels for 0%

commit v1 on v0

--- a/solution.py
+++ b/solution.py
@@ -50,7 +50,9 @@
 def all_blocks(shard, axes, sequence):
     parts = shard[None]
     for k in sequence:
-        parts = lax.all_gather(parts, axes[k], axis=0, tiled=True)
+        parts = jnp.concatenate(
+            lax.all_to_all(jnp.stack([parts] * lax.axis_size(axes[k])), axes[k], 0, 0), axis=0
+        )
     held = [lax.axis_size(axes[k]) for k in reversed(sequence)]
     parts = parts.reshape(*held, *shard.shape)
     turned = sorted(range(len(sequence)), key=lambda place: sequence[len(sequence) - 1 - place])

time: 387 us -> 417 us (1.078)
  waiting for transfers between devices: 149 us -> 175 us
  starting transfers between devices: 23.2 us -> 33.7 us
  blocking collectives: 21.1 us -> 12.8 us
    all_gather x2 -> x0, waiting for transfers between devices: 43.5 us -> none  [all_blocks(): parts = lax.all_gather(parts, axes[k], axis=0, tiled=True)]
    all_to_all x1 -> x2, waiting for transfers between devices: 8.55 us -> 49.4 us  [moved_by_axis(): out = lax.all_to_all(out, axes[k], k, k, tiled=True)]
    all_to_all x0 -> x1, waiting for transfers between devices: none -> 27.7 us  [all_blocks(): lax.all_to_all(jnp.stack([parts] * lax.axis_size(axes[k])), axes[k], 0, 0)]
    all_gather x1 -> x0, blocking collectives: 11.3 us -> none  [all_blocks(): parts = lax.all_gather(parts, axes[k], axis=0, tiled=True)]
    all_to_all x0 -> x1, starting transfers between devices: none -> 7.89 us  [all_blocks(): lax.all_to_all(jnp.stack([parts] * lax.axis_size(axes[k])), axes[k], 0, 0)]
    all_to_all x1 -> x2, blocking collectives: 9.74 us -> 12.8 us  [all_blocks(): lax.all_to_all(jnp.stack([parts] * lax.axis_size(axes[k])), axes[k], 0, 0)]
    all_to_all x1 -> x2, starting transfers between devices: 9.12 us -> 11.8 us  [moved_by_axis(): out = lax.all_to_all(out, axes[k], k, k, tiled=True)]
  transfers between devices with their start and end apart: 8 -> 8, of which waited for: 7 -> 7; matrix products, arithmetic and copies ran while one was open for 3% -> 1% of each run, Pallas kernels for 0% -> 0%
where the time goes in v1:
time: 417 us; the launch traced here: 415 us
  waiting for transfers between devices  175 us (42%)
  matrix products  62.8 us (15%)
  local copies, waits for them, and re-layouts  62.1 us (15%)
  loops' own time  43.6 us (10%)
  starting transfers between devices  33.7 us (8%)
  between operations  16.5 us (4%)
  blocking collectives  12.8 us (3%)
  other arithmetic  8.64 us (2%)
    reduce_scatter x3, waiting for transfers between devices, sum_by_axis(): so_far = lax.psum_scatter(so_far, axis, scatter_dimension=0, tiled=True)  89 us
    dot_general x64, matrix products, one_group(): jnp.einsum('eic,ejc->iej', picked, window, preferred_element_type=jnp.flo...  57.3 us
    all_to_all x2, waiting for transfers between devices, moved_by_axis(): out = lax.all_to_all(out, axes[k], k, k, tiled=True)  49.4 us
    another operation x1, loops' own time, body(): parts = lax.map(one_group, jnp.arange(groups, dtype=jnp.int32))  43.6 us
    dynamic_slice x64, local copies, waits for them, and re-layouts, body(): parts = lax.map(one_group, jnp.arange(groups, dtype=jnp.int32))  37.3 us
    all_to_all x1, waiting for transfers between devices, all_blocks(): lax.all_to_all(jnp.stack([parts] * lax.axis_size(axes[k])), axes[k], 0, 0)  27.7 us
    all_to_all x2, starting transfers between devices, from_everyone(): lax.all_to_all(jnp.broadcast_to(shard[None], (size, *shard.shape)), axis,...  13.9 us
    all_to_all x2, blocking collectives, all_blocks(): lax.all_to_all(jnp.stack([parts] * lax.axis_size(axes[k])), axes[k], 0, 0)  12.8 us
  transfers between devices with their start and end apart: 8, of which 7 were waited for; matrix products, arithmetic and copies ran while one was open for 1% of the time, Pallas kernels for 0%

profile of v1, /device:TPU:1, one launch (start us, length us, event | category | flops | bytes accessed | tf_op | source)
XLA Modules:
  0.0 415.5 jit_solution(1416803030762261976)
XLA Ops:
  7.2 3.6 reshape.315
  10.8 1.2 copy.36
  11.9 1.6 copy.37
  13.5 7.1 %all-to-all-start.3 = ((bf16[32,2,1,32,448]{4,3,0,2,1:T(8,128)(2,1)}), bf16[32,2,1,32,448]{4,3,0,2,1:T(8,128)(2,1)S(1)}, u32[]{:S(2)}, u32[]{:S(2)}) async-start(bf16[32,2,1,32,448]{4,3,0,2,1:T(8,128)(2,1)} %copy.37), calls=%async_computation.3 | async-start | bytes 4194304 | tf_op jit(solution)/shard_map/all_to_all | solution.py:40
  20.6 2.5 all-to-all-done.3
  23.1 7.2 %all_to_all.37 = bf16[4,1,1,32,512]{4,3,2,1,0:T(8,128)(2,1)S(1)} all-to-all(bf16[4,1,1,32,512]{4,3,2,1,0:T(8,128)(2,1)S(1)} %stack.9), channel_id=1, replica_groups=mesh['expert'=4,'shard_0'=8,'shard_1'=4,'shard_2'=2] {'shard_1'}, dimensions={0} | all-to-all | bytes 262144 | tf_op jit(solution)/shard_map/all_to_all | solution.py:54
  30.4 1.1 stack.10
  31.5 7.9 %all-to-all-start.1 = ((bf16[8,4,1,32,512]{4,3,1,2,0:T(8,128)(2,1)}), bf16[8,4,1,32,512]{4,3,1,2,0:T(8,128)(2,1)S(1)}, u32[]{:S(2)}, u32[]{:S(2)}) async-start(bf16[8,4,1,32,512]{4,3,1,2,0:T(8,128)(2,1)} %stack.10), calls=%async_computation.1 | async-start | bytes 2097152 | tf_op jit(solution)/shard_map/all_to_all | solution.py:54
  39.3 1.5 copy.38
  40.8 27.7 %all-to-all-done.1 = bf16[8,4,1,32,512]{4,3,1,2,0:T(8,128)(2,1)S(1)} async-done(((bf16[8,4,1,32,512]{4,3,1,2,0:T(8,128)(2,1)}), bf16[8,4,1,32,512]{4,3,1,2,0:T(8,128)(2,1)S(1)}, u32[]{:S(2)}, u32[]{:S(2)}) %all-to-all-start.1) | async-done | bytes 1048608 | tf_op jit(solution)/shard_map/all_to_all | solution.py:54
  68.7 5.5 %all_to_all.38 = bf16[2,32,1,32,512]{4,3,1,2,0:T(8,128)(2,1)S(1)} all-to-all(bf16[2,32,1,32,512]{4,3,1,2,0:T(8,128)(2,1)S(1)} %pad_maximum_fusion), channel_id=1, replica_groups=mesh['expert'=4,'shard_0'=8,'shard_1'=4,'shard_2'=2] {'shard_2'}, dimensions={0} | all-to-all | bytes 4194304 | tf_op jit(solution)/shard_map/all_to_all | solution.py:54
  74.3 4.8 %all-to-all-start.4 = ((bf16[32,2,1,32,448]{4,3,1,2,0:T(8,128)(2,1)}), bf16[32,2,1,32,448]{4,3,1,2,0:T(8,128)(2,1)}, u32[]{:S(2)}, u32[]{:S(2)}) async-start(bf16[32,2,1,32,448]{4,3,1,2,0:T(8,128)(2,1)} %copy.38), calls=%async_computation.4 | async-start | bytes 4194304 | tf_op jit(solution)/shard_map/all_to_all | solution.py:40
  79.1 1.6 copy.35
  80.7 46.9 %all-to-all-done.4 = bf16[32,2,1,32,448]{4,3,1,2,0:T(8,128)(2,1)} async-done(((bf16[32,2,1,32,448]{4,3,1,2,0:T(8,128)(2,1)}), bf16[32,2,1,32,448]{4,3,1,2,0:T(8,128)(2,1)}, u32[]{:S(2)}, u32[]{:S(2)}) %all-to-all-start.4) | async-done | bytes 1835040 | tf_op jit(solution)/shard_map/all_to_all | solution.py:40
  127.5 3.6 multiply_reduce_fusion
  131.1 4.3 %copy.40 = f32[4,512,448]{1,0,2:T(4,128)} copy(f32[4,512,448]{1,2,0:T(8,128)S(1)} %get-tuple-element.92) | data formatting | bytes 7340032 | tf_op jit(solution)/shard_map/ebik,ebkc->ebic/dot_general | solution.py:100
  135.4 5.5 %reshape.318 = f32[1,2048,448]{1,2,0:T(8,128)} reshape(f32[4,512,448]{1,0,2:T(4,128)} %copy.40) | data formatting | bytes 7340032 | tf_op jit(solution)/shard_map/reshape | solution.py:101
  140.9 3.6 multiply_convert_fusion.1
  144.5 2.8 copy.41
  147.3 138.1 %while.12 = (s32[]{:T(128)}, f32[64,32,1,512]{3,1,2,0:T(8,128)}, s32[64]{0:T(128)S(1)}, bf16[1,2048,448]{2,1,0:T(8,128)(2,1)S(1)}, s32[]{:T(128)}, /*index=5*/s3...) while((s32[]{:T(128)}, f32[64,32,1,512]{3,1,2,0:T(8,128)}, ...), condition=%wide.region_1.0_spmd, body=%wide.region_0.0_spmd.sunk | while | flops 14680088 | bytes 623474 | solution.py:115
  155.0 0.9 fusion.36
  157.2 0.9 fusion.36
  159.4 0.9 fusion.36
  170.2 0.9 fusion.36
  176.6 0.9 fusion.36
  178.8 0.9 fusion.36
  183.1 0.9 fusion.36
  185.3 0.9 fusion.36
  189.6 0.9 fusion.36
  217.6 0.9 fusion.36
  221.9 0.9 fusion.36
  224.1 0.9 fusion.36
  226.3 0.9 fusion.36
  230.6 0.9 fusion.36
  232.8 0.9 fusion.36
  239.2 0.9 fusion.36
  260.8 0.9 fusion.36
  275.9 0.9 fusion.36
  280.2 0.9 fusion.36
  285.5 54.9 %reduce-scatter.4.cloned.1.call-done = f32[256,1,512]{2,0,1:T(8,128)} async-done(((f32[2048,1,512]{2,0,1:T(8,128)}), f32[256,1,512]{2,0,1:T(8,128)}) %reduce-scatter.4.cloned.1.call-update) | async-done | bytes 524304 | tf_op jit(solution)/shard_map/reduce_scatter | solution.py:68
  341.6 4.0 all-to-all-start.5
  345.6 17.8 %reduce-scatter.6.cloned.1.call-done = f32[64,1,512]{2,0,1:T(8,128)} async-done(((f32[256,1,512]{2,0,1:T(8,128)}), f32[64,1,512]{2,0,1:T(8,128)}) %reduce-scatter.6.cloned.1.call-update) | async-done | bytes 131088 | tf_op jit(solution)/shard_map/reduce_scatter | solution.py:68
  365.4 16.3 %reduce-scatter.8.cloned.1.call-done = f32[32,1,512]{2,0,1:T(8,128)} async-done(((f32[64,1,512]{2,0,1:T(8,128)}), f32[32,1,512]{2,0,1:T(8,128)}) %reduce-scatter.8.cloned.1.call-update) | async-done | bytes 65552 | tf_op jit(solution)/shard_map/reduce_scatter | solution.py:68
  381.7 1.6 fusion.12
  383.3 1.4 pad_maximum_fusion.1
  385.2 9.9 %all-to-all-start.6 = ((f32[64,1,2]{2,1,0:T(1,128)}), f32[64,1,2]{2,1,0:T(1,128)S(1)}, u32[]{:S(2)}, u32[]{:S(2)}) async-start(f32[64,1,2]{2,1,0:T(1,128)} %broadcast_in_dim.52), calls=%async_computation.9 | async-start | bytes 65536 | tf_op jit(solution)/shard_map/all_to_all | solution.py:15
  395.1 9.3 %all-to-all-done.6 = f32[64,1,2]{2,1,0:T(1,128)S(1)} async-done(((f32[64,1,2]{2,1,0:T(1,128)}), f32[64,1,2]{2,1,0:T(1,128)S(1)}, u32[]{:S(2)}, u32[]{:S(2)}) %all-to-all-start.6) | async-done | bytes 544 | tf_op jit(solution)/shard_map/all_to_all | solution.py:15
  407.0 2.0 fusion.7
  (135 shorter events, 81.5 us)
Async XLA Ops:
  13.5 7.1 %copy-start = (f32[1,32,512]{2,1,0:T(8,128)S(1)}, f32[1,32,512]{2,1,0:T(8,128)}, u32[]{:S(2)}) copy-start(f32[1,32,512]{2,1,0:T(8,128)} %param.7) | copy-start | bytes 196612
  13.5 9.6 %all-to-all-start.3 = ((bf16[32,2,1,32,448]{4,3,0,2,1:T(8,128)(2,1)}), bf16[32,2,1,32,448]{4,3,0,2,1:T(8,128)(2,1)S(1)}, u32[]{:S(2)}, u32[]{:S(2)}) async-start(bf16[32,2,1,32,448]{4,3,0,2,1:T(8,128)(2,1)} %copy.37), calls=%async_computation.3 | async-start | bytes 4194304 | tf_op jit(solution)/shard_map/all_to_all | solution.py:40
  31.5 37.1 %all-to-all-start.1 = ((bf16[8,4,1,32,512]{4,3,1,2,0:T(8,128)(2,1)}), bf16[8,4,1,32,512]{4,3,1,2,0:T(8,128)(2,1)S(1)}, u32[]{:S(2)}, u32[]{:S(2)}) async-start(bf16[8,4,1,32,512]{4,3,1,2,0:T(8,128)(2,1)} %stack.10), calls=%async_computation.1 | async-start | bytes 2097152 | tf_op jit(solution)/shard_map/all_to_all | solution.py:54
  74.3 53.3 %all-to-all-start.4 = ((bf16[32,2,1,32,448]{4,3,1,2,0:T(8,128)(2,1)}), bf16[32,2,1,32,448]{4,3,1,2,0:T(8,128)(2,1)}, u32[]{:S(2)}, u32[]{:S(2)}) async-start(bf16[32,2,1,32,448]{4,3,1,2,0:T(8,128)(2,1)} %copy.38), calls=%async_computation.4 | async-start | bytes 4194304 | tf_op jit(solution)/shard_map/all_to_all | solution.py:40
  79.0 261.3 %reduce-scatter.4.cloned.1.call-start = ((), (), s32[]{:S(2)}) async-start(), calls=%async_computation.10 | async-start | bytes 4718592 | tf_op jit(solution)/shard_map/reduce_scatter | solution.py:68
  79.1 48.5 %copy-start.1 = (f32[1,448]{1,0:T(1,128)S(1)}, f32[1,448]{1,0:T(1,128)}, u32[]{:S(2)}) copy-start(f32[1,448]{1,0:T(1,128)} %param.8) | copy-start | bytes 5380
  285.4 78.0 %reduce-scatter.6.cloned.1.call-start = ((), (), s32[]{:S(2)}) async-start(), calls=%async_computation.11 | async-start | bytes 655360 | tf_op jit(solution)/shard_map/reduce_scatter | solution.py:68
  341.6 21.9 %all-to-all-start.5 = ((s32[4,1,1]{2,1,0:T(1,128)}), s32[4,1,1]{2,1,0:T(1,128)S(1)}, u32[]{:S(2)}, u32[]{:S(2)}) async-start(s32[4,1,1]{2,1,0:T(1,128)} %broadcast_in_dim.47), calls=%async_computation.8 | async-start | bytes 4096 | tf_op jit(solution)/shard_map/all_to_all | solution.py:15
  345.6 36.1 %reduce-scatter.8.cloned.1.call-start = ((), (), s32[]{:S(2)}) async-start(), calls=%async_computation.12 | async-start | bytes 196608 | tf_op jit(solution)/shard_map/reduce_scatter | solution.py:68
  385.2 19.2 %all-to-all-start.6 = ((f32[64,1,2]{2,1,0:T(1,128)}), f32[64,1,2]{2,1,0:T(1,128)S(1)}, u32[]{:S(2)}, u32[]{:S(2)}) async-start(f32[64,1,2]{2,1,0:T(1,128)} %broadcast_in_dim.52), calls=%async_computation.9 | async-start | bytes 65536 | tf_op jit(solution)/shard_map/all_to_all | solution.py:15
Sparse Core Ops, SparseCore 0:
  285.6 54.7 reduce-scatter.3
  342.9 20.4 reduce-scatter.5
  365.9 15.7 reduce-scatter.7
